TPU v7x, 32 devices: a whole 2x2x4 slice. The times are simulated.
32 devices in a mesh: group: 2 (over y), station: 4 (over z), tm: 2 (over x), chan: 2 (over core).
Axes of the slice: x: 2, y: 2, z: 4, core: 2. Of those that a mesh axis runs over, the one named last changes fastest.
Arguments:
- voltages: bfloat16 [8, 128, 2, 96, 256], P(('group', 'station'), 'chan', None, None, 'tm'), parts along dimension 0, may hold values from -6 to 6
- delays: int32 [8], P(('group', 'station')), parts along dimension 0, may hold values from 0 to 16, as said below
- tap_sets: int32 [8, 128], P(('group', 'station'), 'chan'), parts along dimension 0, may hold values from 0 to 15
- tap_table: bfloat16 [16, 16], replicated, may hold values from -1.5 to 1.5
- weights: bfloat16 [8, 128, 2, 96, 128], P(('group', 'station'), 'chan'), parts along dimension 0, may hold values from -0.3125 to 0.3125
Outputs:
- array_beams: bfloat16 [256, 2, 128, 256], P(('group', 'chan', 'station'), None, None, 'tm'), parts along dimension 0
There are 2 independent parts, one for each index of `group`. A program takes and returns all parts, laid end to end along the dimension named above; an argument that names none is the same for every part. Nothing has to cross between parts.
Inputs may be any that keep to these rules, and one draw needn't show every extreme that they name: `delays`: every delay lies in 0 to 16, and some station has delay 16.
All inputs are finite; a program needn't handle non-finite values.
Results may differ from a plain program's by a relative error of at most 0.0049.
Values may be sent and summed in bfloat16 or wider, within the bound.
A program may use at most 64 MiB of HBM per device.

v0:
```python
import jax
import jax.numpy as jnp
from jax import lax
from jax.sharding import PartitionSpec as P

TAPS = 16
MAXD = 16
BLOCK = 128


def passed_along(value, axis, steps):
    count = lax.axis_size(axis)
    leading, last = (max(0, -steps), min(count, count - steps))
    return lax.ppermute(value, axis, [(source, source + steps) for source in range(leading, last)])


def steering_matrix(weights):
    real_w = weights[:, :, 0]
    imag_w = weights[:, :, 1]
    upper_rows = jnp.concatenate([real_w, imag_w], axis=-1)
    lower_rows = jnp.concatenate([-imag_w, real_w], axis=-1)
    return jnp.concatenate([upper_rows, lower_rows], axis=2)


def body(voltages, delays, tap_sets, tap_table, weights):
    station_number, channel_total, pairing_total, antenna_total, time_length = voltages.shape
    set_count, tap_count = tap_table.shape
    halo_len = MAXD + TAPS - 1
    window_len = BLOCK + halo_len
    flat_voltages = voltages.reshape(
        station_number, channel_total, pairing_total * antenna_total, time_length
    )
    prev_rim = passed_along(flat_voltages[..., time_length - halo_len :], "tm", 1)
    extended = jnp.concatenate([prev_rim, flat_voltages], axis=-1)
    windows = jnp.stack([extended], axis=3)
    set_onehot = (tap_sets[..., None] == jnp.arange(set_count)[None, None, :]).astype(jnp.bfloat16)
    chosen_taps = jnp.einsum(
        "scm,mk->sck", set_onehot, tap_table, preferred_element_type=jnp.float32
    ).astype(jnp.bfloat16)
    window_pos = jnp.arange(window_len)[:, None]
    output_pos = jnp.arange(BLOCK)[None, :]
    lag_table = output_pos + halo_len - window_pos
    station_lag = lag_table[None, :, :] - delays[:, None, None]
    tap_onehot = (station_lag[..., None] == jnp.arange(tap_count)[None, None, None, :]).astype(
        jnp.bfloat16
    )
    band_matrix = jnp.einsum(
        "sck,sjuk->scju", chosen_taps, tap_onehot, preferred_element_type=jnp.float32
    ).astype(jnp.bfloat16)
    delayed_voltages = jnp.einsum(
        "scanj,scju->scanu", windows, band_matrix, preferred_element_type=jnp.float32
    ).astype(jnp.bfloat16)
    delayed_voltages = delayed_voltages.reshape(
        station_number, channel_total, pairing_total * antenna_total, time_length
    )
    station_axis_size = lax.axis_size("station")
    row_count = channel_total // station_axis_size
    split_in = delayed_voltages.reshape(
        station_number, station_axis_size, row_count, pairing_total * antenna_total, time_length
    )
    split_steer = weights.reshape(
        station_number,
        station_axis_size,
        row_count,
        pairing_total,
        antenna_total,
        weights.shape[-1],
    )
    gathered_in = lax.all_to_all(split_in, "station", split_axis=1, concat_axis=0, tiled=True)
    gathered_w = lax.all_to_all(split_steer, "station", split_axis=1, concat_axis=0, tiled=True)
    summed = jnp.einsum(
        "scan,scat->cnt",
        steering_matrix(gathered_w[:, 0]),
        gathered_in[:, 0],
        preferred_element_type=jnp.float32,
    )
    beam_count = weights.shape[-1]
    return summed.astype(jnp.bfloat16).reshape(row_count, 2, beam_count, time_length)


def solution(mesh):
    return jax.shard_map(
        body,
        mesh=mesh,
        in_specs=(
            P(("group", "station"), "chan", None, None, "tm"),
            P(("group", "station")),
            P(("group", "station"), "chan"),
            P(),
            P(("group", "station"), "chan", None, None, None),
        ),
        out_specs=P(("group", "chan", "station"), None, None, "tm"),
        check_vma=False,
    )
```

profile of v0, /device:TPU:0, one launch (start us, length us, event | category | flops | bytes accessed | tf_op | source)
XLA Modules:
  0.0 160.1 jit_solution(11267425315163392430)
XLA Ops:
  0.0 0.0 copy-start
  0.0 3.9 %copy.12 = bf16[1,4,16,2,96,128]{5,4,2,3,0,1:T(8,128)(2,1)} copy(bf16[1,4,16,2,96,128]{5,4,3,2,1,0:T(8,128)(2,1)} %bitcast.40) | data formatting | bytes 6291456 | tf_op jit(solution)/shard_map/reshape | solution.py:61
  3.9 0.0 copy-start.1
  3.9 6.6 %all-to-all-start = ((bf16[1,4,16,2,96,128]{5,4,2,3,0,1:T(8,128)(2,1)}), bf16[1,4,16,2,96,128]{5,4,2,3,0,1:T(8,128)(2,1)}, u32[]{:S(2)}, u32[]{:S(2)}) async-start(bf16[1,4,16,2,96,128]{5,4,2,3,0,1:T(8,128)(2,1)} %copy.12), calls=%async_computation | async-start | bytes 6291456 | tf_op jit(solution)/shard_map/all_to_all | solution.py:70
  10.5 0.0 copy-done.1
  10.6 2.6 %slice.14 = bf16[1,64,192,31]{3,2,1,0:T(8,128)(2,1)} slice(bf16[1,64,192,128]{3,2,1,0:T(8,128)(2,1)S(1)} %bitcast.38), slice={[0:1], [0:64], [0:192], [97:128]} | slice | bytes 1523712 | tf_op jit(solution)/shard_map/slice | solution.py:33
  13.2 4.4 %copy.14 = bf16[1,64,192,31]{2,1,3,0:T(8,128)(2,1)} copy(bf16[1,64,192,31]{3,2,1,0:T(8,128)(2,1)} %slice.14) | data formatting | bytes 1523712 | tf_op jit(solution)/shard_map/slice | solution.py:33
  17.6 0.0 copy-start.2
  17.6 4.5 %collective-permute-start = (bf16[1,64,192,31]{2,1,3,0:T(8,128)(2,1)}, bf16[1,64,192,31]{2,1,3,0:T(8,128)(2,1)}, u32[]{:S(2)}, u32[]{:S(2)}) collective-permute-start(bf16[1,64,192,31]{2,1,3,0:T(8,128)(2,1)} %copy.14), channel_id=1, source_target_pairs={{0,2},{1,3},{4,6},{5,7},{8,10},{9,11},{12,14},{13,15},{16,18},{17,... | collective-permute-start | bytes 2285576 | tf_op jit(solution)/shard_map/ppermute | solution.py:14
  22.1 4.8 %copy.16 = bf16[1,64,192,128]{2,3,1,0:T(8,128)(2,1)} copy(bf16[1,64,192,128]{3,2,1,0:T(8,128)(2,1)S(1)} %bitcast.39) | data formatting | bytes 6291456 | tf_op jit(solution)/shard_map/reshape | solution.py:30
  27.6 0.0 copy-done
  27.6 0.0 copy-done.2
  27.6 1.1 convolution_convert_fusion
  28.7 14.2 %collective-permute-done = bf16[1,64,192,31]{2,1,3,0:T(8,128)(2,1)} collective-permute-done((bf16[1,64,192,31]{2,1,3,0:T(8,128)(2,1)}, bf16[1,64,192,31]{2,1,3,0:T(8,128)(2,1)}, u32[]{:S(2)}, u32[]{:S(2)}) %collective-permute-start) | collective-permute-done | bytes 761888 | tf_op jit(solution)/shard_map/ppermute | solution.py:14
  42.9 1.8 %copy.15 = bf16[1,64,192,31]{2,3,1,0:T(8,128)(2,1)S(1)} copy(bf16[1,64,192,31]{2,1,3,0:T(8,128)(2,1)} %collective-permute-done) | data formatting | bytes 1523712 | tf_op jit(solution)/shard_map/ppermute | solution.py:14
  44.7 8.7 %fusion.14 = bf16[64,192,128]{2,1,0:T(8,128)(2,1)} fusion(bf16[64,159,128]{2,0,1:T(8,128)(2,1)S(1)} %convolution_convert_fusion, bf16[1,64,192,128]{2,3,1,0:T(8,128)(2,1)} %copy.16, bf16[1,64,192,31]{2,3,1,0:T(8,128)(2,1)S(1)} %copy.15), kind=kOutput, calls=%fused_computation.16 | convolution fusion | flops 509558784 | bytes 9658368 | tf_op jit(solution)/shard_map/scanj,scju->scanu/dot_general | solution.py:50
  53.4 27.9 %all-to-all-done = bf16[1,4,16,2,96,128]{5,4,2,3,0,1:T(8,128)(2,1)} async-done(((bf16[1,4,16,2,96,128]{5,4,2,3,0,1:T(8,128)(2,1)}), bf16[1,4,16,2,96,128]{5,4,2,3,0,1:T(8,128)(2,1)}, u32[]{:S(2)}, u32[]{:S(2)}) %all-to-all-start) | async-done | bytes 3145760 | tf_op jit(solution)/shard_map/all_to_all | solution.py:70
  81.3 3.7 %all-to-all-start.1 = ((bf16[1,4,16,192,128]{4,3,2,0,1:T(8,128)(2,1)}), bf16[1,4,16,192,128]{4,3,2,0,1:T(8,128)(2,1)S(1)}, u32[]{:S(2)}, u32[]{:S(2)}) async-start(bf16[1,4,16,192,128]{4,3,2,0,1:T(8,128)(2,1)} %bitcast.10), calls=%async_computation.1 | async-start | bytes 6291456 | tf_op jit(solution)/shard_map/all_to_all | solution.py:69
  85.0 2.3 %copy.32 = bf16[1,4,16,2,96,128]{5,4,1,2,3,0:T(8,128)(2,1)S(1)} copy(bf16[1,4,16,2,96,128]{5,4,2,3,0,1:T(8,128)(2,1)} %all-to-all-done) | data formatting | bytes 6291456 | tf_op jit(solution)/shard_map/all_to_all | solution.py:70
  87.3 1.4 fusion.27
  88.7 2.0 %slice_bitcast_fusion = (bf16[4,16,96,128]{3,2,0,1:T(8,128)(2,1)}, bf16[4,16,96,128]{3,2,0,1:T(8,128)(2,1)}) fusion(bf16[4,16,2,96,128]{4,3,0,1,2:T(8,128)(2,1)S(1)} %bitcast.37), kind=kLoop, calls=%fused_computation.19 | loop fusion | bytes 6291456 | tf_op jit(solution)/shard_map/squeeze | solution.py:19
  90.7 64.4 %all-to-all-done.1 = bf16[1,4,16,192,128]{4,3,2,0,1:T(8,128)(2,1)S(1)} async-done(((bf16[1,4,16,192,128]{4,3,2,0,1:T(8,128)(2,1)}), bf16[1,4,16,192,128]{4,3,2,0,1:T(8,128)(2,1)S(1)}, u32[]{:S(2)}, u32[]{:S(2)}) %all-to-all-start.1) | async-done | bytes 3145760 | tf_op jit(solution)/shard_map/all_to_all | solution.py:69
  155.1 4.9 %bitcast_convert_fusion = bf16[16,256,128]{2,1,0:T(8,128)(2,1)} fusion(bf16[1,4,16,192,128]{4,3,2,0,1:T(8,128)(2,1)S(1)} %all-to-all-done.1, bf16[4,16,96,128]{3,2,0,1:T(8,128)(2,1)} %get-tuple-element.6, bf16[4,16,96,128]{3,2,0,1:T(8,128)(2,1)} %fusion.27, bf16[4,16,96,128]{3,2,0,1:T(8,128)(2,1)} %get-tuple-element.5), kind=kOutput, calls=%fused_computation.17 | convolution fusion | flops 830996480 | bytes 8912896 | tf_op jit(solution)/shard_map/scan,scat->cnt/dot_general | solution.py:71
  (2 shorter events, 0.0 us)
Async XLA Ops:
  0.0 27.6 %copy-start = (bf16[16,16]{1,0:T(8,128)(2,1)S(1)}, bf16[16,16]{1,0:T(8,128)(2,1)}, u32[]{:S(2)}) copy-start(bf16[16,16]{1,0:T(8,128)(2,1)} %param.8) | copy-start | bytes 1540
  3.9 6.6 %copy-start.1 = (bf16[1,64,2,96,128]{4,3,2,1,0:T(8,128)(2,1)S(1)}, bf16[1,64,2,96,128]{4,3,2,1,0:T(8,128)(2,1)}, u32[]{:S(2)}) copy-start(bf16[1,64,2,96,128]{4,3,2,1,0:T(8,128)(2,1)} %param.5) | copy-start | bytes 9437188
  3.9 77.4 %all-to-all-start = ((bf16[1,4,16,2,96,128]{5,4,2,3,0,1:T(8,128)(2,1)}), bf16[1,4,16,2,96,128]{5,4,2,3,0,1:T(8,128)(2,1)}, u32[]{:S(2)}, u32[]{:S(2)}) async-start(bf16[1,4,16,2,96,128]{5,4,2,3,0,1:T(8,128)(2,1)} %copy.12), calls=%async_computation | async-start | bytes 6291456 | tf_op jit(solution)/shard_map/all_to_all | solution.py:70
  17.6 10.0 %copy-start.2 = (s32[1,64]{1,0:T(1,128)S(1)}, s32[1,64]{1,0:T(1,128)}, u32[]{:S(2)}) copy-start(s32[1,64]{1,0:T(1,128)} %param.7) | copy-start | bytes 772
  17.6 25.3 %collective-permute-start = (bf16[1,64,192,31]{2,1,3,0:T(8,128)(2,1)}, bf16[1,64,192,31]{2,1,3,0:T(8,128)(2,1)}, u32[]{:S(2)}, u32[]{:S(2)}) collective-permute-start(bf16[1,64,192,31]{2,1,3,0:T(8,128)(2,1)} %copy.14), channel_id=1, source_target_pairs={{0,2},{1,3},{4,6},{5,7},{8,10},{9,11},{12,14},{13,15},{16,18},{17,... | collective-permute-start | bytes 2285576 | tf_op jit(solution)/shard_map/ppermute | solution.py:14
  81.3 73.8 %all-to-all-start.1 = ((bf16[1,4,16,192,128]{4,3,2,0,1:T(8,128)(2,1)}), bf16[1,4,16,192,128]{4,3,2,0,1:T(8,128)(2,1)S(1)}, u32[]{:S(2)}, u32[]{:S(2)}) async-start(bf16[1,4,16,192,128]{4,3,2,0,1:T(8,128)(2,1)} %bitcast.10), calls=%async_computation.1 | async-start | bytes 6291456 | tf_op jit(solution)/shard_map/all_to_all | solution.py:69
where the time goes:
time: 161 us; the launch traced here: 160 us
  waiting for transfers between devices  107 us (66%)
  local copies, waits for them, and re-layouts  21.9 us (14%)
  starting transfers between devices  14.8 us (9%)
  matrix products  14.7 us (9%)
    all_to_all x1, waiting for transfers between devices, body(): lax.all_to_all(split_in, 'station', split_axis=1, concat_axis=0, tiled=True)  64.4 us
    all_to_all x1, waiting for transfers between devices, body(): lax.all_to_all(split_steer, 'station', split_axis=1, concat_axis=0, tiled...  27.9 us
    ppermute x1, waiting for transfers between devices, passed_along(): lax.ppermute(value, axis, [(source, source + steps) for source in range(l...  14.2 us
    dot_general x1, matrix products, body(): jnp.einsum('scanj,scju->scanu', windows, band_matrix, preferred_element_t...  8.68 us
    slice x2, local copies, waits for them, and re-layouts, body(): flat_voltages[..., time_length - halo_len:]  7.05 us
    all_to_all x1, starting transfers between devices, body(): lax.all_to_all(split_steer, 'station', split_axis=1, concat_axis=0, tiled...  6.61 us
    dot_general x1, matrix products, body(): jnp.einsum('scan,scat->cnt', steering_matrix(gathered_w[:, 0]), gathered_...  4.93 us
    reshape x1, local copies, waits for them, and re-layouts, body(): voltages.reshape(station_number, channel_total, pairing_total * antenna_t...  4.84 us
  transfers between devices with their start and end apart: 3, of which 3 were waited for; matrix products, arithmetic and copies ran while one was open for 18% of the time, Pallas kernels for 0%

commit v1 on v0

--- a/solution.py
+++ b/solution.py
@@ -67,7 +67,12 @@
         weights.shape[-1],
     )
     gathered_in = lax.all_to_all(split_in, "station", split_axis=1, concat_axis=0, tiled=True)
-    gathered_w = lax.all_to_all(split_steer, "station", split_axis=1, concat_axis=0, tiled=True)
+    gathered_w = jnp.concatenate(
+        lax.all_to_all(
+            jnp.stack(jnp.split(split_steer, lax.axis_size("station"), axis=1)), "station", 0, 0
+        ),
+        axis=0,
+    )
     summed = jnp.einsum(
         "scan,scat->cnt",
         steering_matrix(gathered_w[:, 0]),

time: 161 us -> 161 us (level)
    another operation x0 -> x2, local copies, waits for them, and re-layouts: none -> 4.08 us  [body(): jnp.stack(jnp.split(split_steer, lax.axis_size('station'), axis=1))]
    reshape x1 -> x0, local copies, waits for them, and re-layouts: 3.93 us -> none  [body(): weights.reshape(station_number, station_axis_size, row_count, pairing_tot...]
where the time goes in v1:
time: 161 us
  waiting for transfers between devices  107 us (66%)
  local copies, waits for them, and re-layouts  22.1 us (14%)
  starting transfers between devices  14.8 us (9%)
  matrix products  14.7 us (9%)
  other arithmetic  1.83 us (1%)
    all_to_all x1, waiting for transfers between devices, body(): lax.all_to_all(split_in, 'station', split_axis=1, concat_axis=0, tiled=True)  64.4 us
    all_to_all x1, waiting for transfers between devices, body(): lax.all_to_all(jnp.stack(jnp.split(split_steer, lax.axis_size('station'),...  27.9 us
    ppermute x1, waiting for transfers between devices, passed_along(): lax.ppermute(value, axis, [(source, source + steps) for source in range(l...  14.2 us
    dot_general x1, matrix products, body(): jnp.einsum('scanj,scju->scanu', windows, band_matrix, preferred_element_t...  8.69 us
    slice x2, local copies, waits for them, and re-layouts, body(): flat_voltages[..., time_length - halo_len:]  7.05 us
    all_to_all x1, starting transfers between devices, body(): lax.all_to_all(jnp.stack(jnp.split(split_steer, lax.axis_size('station'),...  6.61 us
    dot_general x1, matrix products, body(): jnp.einsum('scan,scat->cnt', steering_matrix(gathered_w[:, 0]), gathered_...  4.93 us
    reshape x1, local copies, waits for them, and re-layouts, body(): voltages.reshape(station_number, channel_total, pairing_total * antenna_t...  4.87 us
  transfers between devices with their start and end apart: 3, of which 3 were waited for; matrix products, arithmetic and copies ran while one was open for 18% of the time, Pallas kernels for 0%

profile of v1, /device:TPU:0, one launch (start us, length us, event | category | flops | bytes accessed | tf_op | source)
XLA Modules:
  0.0 160.7 jit_solution(4297086752229704053)
XLA Ops:
  0.0 0.0 copy-start
  0.0 2.1 %slice_bitcast_fusion.5 = (bf16[1,1,1,16,2,96,128]{6,5,4,3,2,1,0:T(8,128)(2,1)S(1)}, bf16[1,1,1,16,2,96,128]{6,5,4,3,2,1,0:T(8,128)(2,1)S(1)}, bf16[1,1,1,16,2,9...) fusion(bf16[1,4,16,2,96,128]{5,4,3,2,1,0:T(8,128)(2,1)} %bitcast.48), kind=kLoop, calls=%fused_computation.28 | loop fusion | bytes 6291456 | tf_op jit(solution)/shard_map/stack | solution.py:72
  2.1 0.4 pad_maximum_fusion
  2.5 2.0 %copy.18 = bf16[4,1,1,16,2,96,128]{6,5,3,4,2,1,0:T(8,128)(2,1)} copy(bf16[4,1,1,16,2,96,128]{6,5,4,3,2,1,0:T(8,128)(2,1)S(1)} %pad_maximum_fusion) | data formatting | bytes 6291456 | tf_op jit(solution)/shard_map/stack | solution.py:72
  4.5 0.0 copy-start.1
  4.5 6.6 %all-to-all-start = ((bf16[4,1,1,16,2,96,128]{6,5,3,4,2,1,0:T(8,128)(2,1)}), bf16[4,1,1,16,2,96,128]{6,5,3,4,2,1,0:T(8,128)(2,1)}, u32[]{:S(2)}, u32[]{:S(2)}) async-start(bf16[4,1,1,16,2,96,128]{6,5,3,4,2,1,0:T(8,128)(2,1)} %copy.18), calls=%async_computation | async-start | bytes 6291456 | tf_op jit(solution)/shard_map/all_to_all | solution.py:71
  11.2 0.0 copy-done.1
  11.2 2.6 %slice.14 = bf16[1,64,192,31]{3,2,1,0:T(8,128)(2,1)} slice(bf16[1,64,192,128]{3,2,1,0:T(8,128)(2,1)S(1)} %bitcast.46), slice={[0:1], [0:64], [0:192], [97:128]} | slice | bytes 1523712 | tf_op jit(solution)/shard_map/slice | solution.py:33
  13.8 4.4 %copy.20 = bf16[1,64,192,31]{2,1,3,0:T(8,128)(2,1)} copy(bf16[1,64,192,31]{3,2,1,0:T(8,128)(2,1)} %slice.14) | data formatting | bytes 1523712 | tf_op jit(solution)/shard_map/slice | solution.py:33
  18.2 0.0 copy-start.2
  18.2 4.5 %collective-permute-start = (bf16[1,64,192,31]{2,1,3,0:T(8,128)(2,1)}, bf16[1,64,192,31]{2,1,3,0:T(8,128)(2,1)}, u32[]{:S(2)}, u32[]{:S(2)}) collective-permute-start(bf16[1,64,192,31]{2,1,3,0:T(8,128)(2,1)} %copy.20), channel_id=1, source_target_pairs={{0,2},{1,3},{4,6},{5,7},{8,10},{9,11},{12,14},{13,15},{16,18},{17,... | collective-permute-start | bytes 2285576 | tf_op jit(solution)/shard_map/ppermute | solution.py:14
  22.7 4.9 %copy.22 = bf16[1,64,192,128]{2,3,1,0:T(8,128)(2,1)} copy(bf16[1,64,192,128]{3,2,1,0:T(8,128)(2,1)S(1)} %bitcast.47) | data formatting | bytes 6291456 | tf_op jit(solution)/shard_map/reshape | solution.py:30
  28.3 0.0 copy-done
  28.3 0.0 copy-done.2
  28.3 1.1 convolution_convert_fusion
  29.4 14.2 %collective-permute-done = bf16[1,64,192,31]{2,1,3,0:T(8,128)(2,1)} collective-permute-done((bf16[1,64,192,31]{2,1,3,0:T(8,128)(2,1)}, bf16[1,64,192,31]{2,1,3,0:T(8,128)(2,1)}, u32[]{:S(2)}, u32[]{:S(2)}) %collective-permute-start) | collective-permute-done | bytes 761888 | tf_op jit(solution)/shard_map/ppermute | solution.py:14
  43.5 1.8 %copy.21 = bf16[1,64,192,31]{2,3,1,0:T(8,128)(2,1)S(1)} copy(bf16[1,64,192,31]{2,1,3,0:T(8,128)(2,1)} %collective-permute-done) | data formatting | bytes 1523712 | tf_op jit(solution)/shard_map/ppermute | solution.py:14
  45.3 8.7 %fusion.14 = bf16[64,192,128]{2,1,0:T(8,128)(2,1)} fusion(bf16[64,159,128]{2,0,1:T(8,128)(2,1)S(1)} %convolution_convert_fusion, bf16[1,64,192,128]{2,3,1,0:T(8,128)(2,1)} %copy.22, bf16[1,64,192,31]{2,3,1,0:T(8,128)(2,1)S(1)} %copy.21), kind=kOutput, calls=%fused_computation.17 | convolution fusion | flops 509558784 | bytes 9658368 | tf_op jit(solution)/shard_map/scanj,scju->scanu/dot_general | solution.py:50
  54.0 27.9 %all-to-all-done = bf16[4,1,1,16,2,96,128]{6,5,3,4,2,1,0:T(8,128)(2,1)} async-done(((bf16[4,1,1,16,2,96,128]{6,5,3,4,2,1,0:T(8,128)(2,1)}), bf16[4,1,1,16,2,96,128]{6,5,3,4,2,1,0:T(8,128)(2,1)}, u32[]{:S(2)}, u32[]{:S(2)}) %all-to-all-start) | async-done | bytes 3145760 | tf_op jit(solution)/shard_map/all_to_all | solution.py:71
  81.9 3.7 %all-to-all-start.1 = ((bf16[1,4,16,192,128]{4,3,2,0,1:T(8,128)(2,1)}), bf16[1,4,16,192,128]{4,3,2,0,1:T(8,128)(2,1)S(1)}, u32[]{:S(2)}, u32[]{:S(2)}) async-start(bf16[1,4,16,192,128]{4,3,2,0,1:T(8,128)(2,1)} %bitcast.14), calls=%async_computation.1 | async-start | bytes 6291456 | tf_op jit(solution)/shard_map/all_to_all | solution.py:69
  85.6 2.3 %copy.38 = bf16[4,1,1,16,2,96,128]{6,5,0,3,4,2,1:T(8,128)(2,1)S(1)} copy(bf16[4,1,1,16,2,96,128]{6,5,3,4,2,1,0:T(8,128)(2,1)} %all-to-all-done) | data formatting | bytes 6291456 | tf_op jit(solution)/shard_map/all_to_all | solution.py:71
  87.9 1.4 fusion.27
  89.3 2.0 %slice_bitcast_fusion = (bf16[4,16,96,128]{3,2,0,1:T(8,128)(2,1)}, bf16[4,16,96,128]{3,2,0,1:T(8,128)(2,1)}) fusion(bf16[4,16,2,96,128]{4,3,0,1,2:T(8,128)(2,1)S(1)} %bitcast.45), kind=kLoop, calls=%fused_computation.20 | loop fusion | bytes 6291456 | tf_op jit(solution)/shard_map/squeeze | solution.py:19
  91.3 64.4 %all-to-all-done.1 = bf16[1,4,16,192,128]{4,3,2,0,1:T(8,128)(2,1)S(1)} async-done(((bf16[1,4,16,192,128]{4,3,2,0,1:T(8,128)(2,1)}), bf16[1,4,16,192,128]{4,3,2,0,1:T(8,128)(2,1)S(1)}, u32[]{:S(2)}, u32[]{:S(2)}) %all-to-all-start.1) | async-done | bytes 3145760 | tf_op jit(solution)/shard_map/all_to_all | solution.py:69
  155.7 4.9 %bitcast_convert_fusion = bf16[16,256,128]{2,1,0:T(8,128)(2,1)} fusion(bf16[1,4,16,192,128]{4,3,2,0,1:T(8,128)(2,1)S(1)} %all-to-all-done.1, bf16[4,16,96,128]{3,2,0,1:T(8,128)(2,1)} %get-tuple-element.6, bf16[4,16,96,128]{3,2,0,1:T(8,128)(2,1)} %fusion.27, bf16[4,16,96,128]{3,2,0,1:T(8,128)(2,1)} %get-tuple-element.5), kind=kOutput, calls=%fused_computation.18 | convolution fusion | flops 830996480 | bytes 8912896 | tf_op jit(solution)/shard_map/scan,scat->cnt/dot_general | solution.py:76
  (2 shorter events, 0.0 us)
Async XLA Ops:
  0.0 28.3 %copy-start = (bf16[16,16]{1,0:T(8,128)(2,1)S(1)}, bf16[16,16]{1,0:T(8,128)(2,1)}, u32[]{:S(2)}) copy-start(bf16[16,16]{1,0:T(8,128)(2,1)} %param.8) | copy-start | bytes 1540
  4.5 6.6 %copy-start.1 = (bf16[1,64,2,96,128]{4,3,2,1,0:T(8,128)(2,1)S(1)}, bf16[1,64,2,96,128]{4,3,2,1,0:T(8,128)(2,1)}, u32[]{:S(2)}) copy-start(bf16[1,64,2,96,128]{4,3,2,1,0:T(8,128)(2,1)} %param.5) | copy-start | bytes 9437188
  4.5 77.4 %all-to-all-start = ((bf16[4,1,1,16,2,96,128]{6,5,3,4,2,1,0:T(8,128)(2,1)}), bf16[4,1,1,16,2,96,128]{6,5,3,4,2,1,0:T(8,128)(2,1)}, u32[]{:S(2)}, u32[]{:S(2)}) async-start(bf16[4,1,1,16,2,96,128]{6,5,3,4,2,1,0:T(8,128)(2,1)} %copy.18), calls=%async_computation | async-start | bytes 6291456 | tf_op jit(solution)/shard_map/all_to_all | solution.py:71
  18.2 10.1 %copy-start.2 = (s32[1,64]{1,0:T(1,128)S(1)}, s32[1,64]{1,0:T(1,128)}, u32[]{:S(2)}) copy-start(s32[1,64]{1,0:T(1,128)} %param.7) | copy-start | bytes 772
  18.2 25.3 %collective-permute-start = (bf16[1,64,192,31]{2,1,3,0:T(8,128)(2,1)}, bf16[1,64,192,31]{2,1,3,0:T(8,128)(2,1)}, u32[]{:S(2)}, u32[]{:S(2)}) collective-permute-start(bf16[1,64,192,31]{2,1,3,0:T(8,128)(2,1)} %copy.20), channel_id=1, source_target_pairs={{0,2},{1,3},{4,6},{5,7},{8,10},{9,11},{12,14},{13,15},{16,18},{17,... | collective-permute-start | bytes 2285576 | tf_op jit(solution)/shard_map/ppermute | solution.py:14
  81.9 73.8 %all-to-all-start.1 = ((bf16[1,4,16,192,128]{4,3,2,0,1:T(8,128)(2,1)}), bf16[1,4,16,192,128]{4,3,2,0,1:T(8,128)(2,1)S(1)}, u32[]{:S(2)}, u32[]{:S(2)}) async-start(bf16[1,4,16,192,128]{4,3,2,0,1:T(8,128)(2,1)} %bitcast.14), calls=%async_computation.1 | async-start | bytes 6291456 | tf_op jit(solution)/shard_map/all_to_all | solution.py:69
